TPU v7x, 32 devices: a whole 2x2x4 slice. The times are simulated.
32 devices in a mesh: dp: 4 (over y, x), tp: 8 (over z, core).
Axes of the slice: x: 2, y: 2, z: 4, core: 2. Of those that a mesh axis runs over, the one named last changes fastest.
Arguments:
- gradients: bfloat16 [4, 4, 3072, 768], P('dp', None, 'tp'), may hold values from -6 to 6, as said below
- right_factor: float32 [4, 768, 8], replicated, may hold values from -6 to 6
- weights_before: float32 [4, 3072, 768], P(None, 'tp', 'dp'), may hold values from -0.21875 to 0.21875
- momentum: float32 [4, 3072, 768], P(None, 'tp', 'dp'), may hold values from -0.3125 to 0.3125
Outputs:
- new_weights: float32 [4, 3072, 768], P(None, 'tp', 'dp')
- new_basis: float32 [4, 768, 8], replicated
- new_momentum: float32 [4, 3072, 768], P(None, 'tp', 'dp')
Inputs may be any that keep to these rules, and one draw needn't show every extreme that they name: gradients holds numbers from -6 to 6.
All inputs are finite; a program needn't handle non-finite values.
Results may differ from a plain program's by a relative error of at most 0.0003.
Values sent between devices are 32-bit elements.
A program may use at most 64 MiB of HBM per device.

v0:
```python
import jax
import jax.numpy as jnp
from jax import lax
from jax.sharding import PartitionSpec as P

RANK = 8


def on_device(gradients, right_factor, weights_before, momentum):
    own_grads = gradients[0]
    part_left = jnp.einsum(
        "liw,lwr->lir",
        own_grads,
        right_factor.astype(jnp.bfloat16),
        preferred_element_type=jnp.float32,
    )
    left = lax.psum(part_left, "dp")
    part_gram = jnp.einsum("lir,lis->lrs", left, left, precision=lax.Precision.HIGHEST)
    small_left = left.astype(jnp.bfloat16)
    part_right = jnp.einsum(
        "liw,lir->lwr", own_grads, small_left, preferred_element_type=jnp.float32
    )
    own_share = part_gram / lax.axis_size("dp")
    right, gram = lax.psum((part_right, own_share), ("dp", "tp"))
    gram = gram + 0.001 * jnp.mean(jnp.diagonal(gram, axis1=1, axis2=2), axis=1)[
        :, None, None
    ] * jnp.eye(RANK, dtype=jnp.float32)
    place = lax.axis_index("dp") * weights_before.shape[2]
    own_right = lax.dynamic_slice_in_dim(right, place, weights_before.shape[2], axis=1)
    root = jnp.linalg.cholesky(gram)
    half = lax.linalg.triangular_solve(
        root, jnp.swapaxes(own_right, 1, 2), left_side=True, lower=True
    )
    mixed = lax.linalg.triangular_solve(root, half, left_side=True, lower=True, transpose_a=True)
    change = jnp.einsum(
        "lir,lrw->liw", left, mixed, precision=lax.Precision.HIGHEST
    ) / lax.axis_size("dp")
    new_momentum = 0.9 * momentum + change
    new_weights = weights_before - 0.02 * new_momentum
    new_basis = right * lax.rsqrt(jnp.mean(right * right, axis=(1, 2), keepdims=True) + 1e-12)
    return (new_weights, new_basis, new_momentum)


def solution(mesh):
    in_specs = (P("dp", None, "tp", None), P(), P(None, "tp", "dp"), P(None, "tp", "dp"))
    out_specs = (P(None, "tp", "dp"), P(), P(None, "tp", "dp"))
    return jax.shard_map(
        on_device, mesh=mesh, in_specs=in_specs, out_specs=out_specs, check_vma=False
    )
```

profile of v0, /device:TPU:8, one launch (start us, length us, event | category | flops | bytes accessed | tf_op | source)
XLA Modules:
  0.0 166.5 jit_solution(5481928536512770521)
XLA Ops:
  7.2 0.0 copy-start
  7.2 0.0 all-reduce.2.cloned.1.call-start
  7.2 1.6 copy-done
  8.8 1.6 fusion.2
  10.4 16.7 %psum.21 = f32[4,384,8]{1,2,0:T(8,128)S(1)} all-reduce(f32[4,384,8]{1,2,0:T(8,128)S(1)} %fusion.2), channel_id=1, replica_groups=mesh['dp'=4,'tp'=8] {'dp'}, use_global_device_ids=true, to_apply=%region_0.0 | all-reduce | flops 12288 | bytes 98304 | tf_op jit(solution)/shard_map/psum | solution.py:17
  27.1 1.1 fusion.5
  28.2 0.0 all-reduce.2.cloned.1.call-update
  28.3 0.2 convolution_multiply_fusion.1
  28.5 0.1 copy.13
  28.5 39.5 %psum.22 = f32[4,8,8]{1,2,0:T(8,128)S(1)} all-reduce(f32[4,8,8]{1,2,0:T(8,128)S(1)} %convolution_multiply_fusion.1), channel_id=1, replica_groups=mesh['dp'=4,'tp'=8] {'dp','tp'}, use_global_device_ids=true, to_apply=%region_1.0 | all-reduce | flops 256 | bytes 2048 | tf_op jit(solution)/shard_map/psum | solution.py:24
  68.0 0.1 copy.12
  68.1 0.6 gather_fusion
  68.7 0.1 multiply_add_fusion
  68.8 0.1 copy.14
  68.9 0.1 fusion.15
  69.0 2.9 %custom-call.9 = f32[4,8,8]{2,1,0:T(8,128)S(1)} custom-call(f32[4,8,8]{2,1,0:T(8,128)S(1)} %fusion.15), custom_call_target="Cholesky" | custom-call | tf_op jit(solution)/shard_map/jit(cholesky)/cholesky | solution.py:30
  71.9 0.1 select_reduce_fusion
  71.9 0.1 compare_reduce_fusion
  72.0 0.1 select_bitcast_fusion
  72.1 2.5 %custom-call.10 = f32[4,1,8,8]{2,3,1,0:T(8,128)S(1)} custom-call(f32[4,1,8,8]{3,2,1,0:T(8,128)S(1)} %select_bitcast_fusion), custom_call_target="InvertDiagBlocksLowerTriangular" | custom-call | tf_op jit(solution)/shard_map/triangular_solve | solution.py:34
  74.6 77.7 %all-reduce.2.cloned.1.call-done = f32[4,768,8]{1,2,0:T(8,128)} async-done(((f32[4,768,8]{1,2,0:T(8,128)}), f32[4,768,8]{1,2,0:T(8,128)}) %all-reduce.2.cloned.1.call-update) | async-done | bytes 98320 | tf_op jit(solution)/shard_map/psum | solution.py:24
  152.3 1.0 multiply_reduce_fusion
  153.3 1.1 fusion.9
  154.4 0.2 fusion.12
  154.5 0.0 copy-start.1
  154.5 4.4 %multiply_subtract_fusion = (f32[4,384,192]{1,2,0:T(8,128)}, f32[4,384,192]{1,2,0:T(8,128)}) fusion(f32[4,384,192]{1,2,0:T(8,128)} %param.6, f32[4,384,8]{1,2,0:T(8,128)S(1)} %psum.21, f32[4,8,192]{2,1,0:T(8,128)S(1)} %fusion.12, f32[4,384,192]{1,2,0:T(8,128)} %param.7), kind=kOutput, calls=%fused_computation.7 | convolution fusion | flops 29786112 | bytes 4792320 | tf_op jit(solution)/shard_map/lir,lrw->liw/dot_general | solution.py:35
  158.9 0.0 copy-done.1
  158.9 0.7 broadcast_multiply_fusion
  (7 shorter events, 0.1 us)
Async XLA Ops:
  7.2 1.7 %copy-start = (bf16[1,4,384,768]{3,2,1,0:T(8,128)(2,1)S(1)}, bf16[1,4,384,768]{3,2,1,0:T(8,128)(2,1)}, u32[]{:S(2)}) copy-start(bf16[1,4,384,768]{3,2,1,0:T(8,128)(2,1)} %param.4) | copy-start | bytes 7077892
  7.2 145.1 %all-reduce.2.cloned.1.call-start = ((), (), s32[]{:S(2)}) async-start(), calls=%async_computation | async-start | bytes 196608 | tf_op jit(solution)/shard_map/psum | solution.py:24
  154.5 4.4 %copy-start.1 = (f32[4,768,8]{1,2,0:T(8,128)S(1)}, f32[4,768,8]{1,2,0:T(8,128)}, u32[]{:S(2)}) copy-start(f32[4,768,8]{1,2,0:T(8,128)} %all-reduce.2.cloned.1.call-done) | copy-start | bytes 294916
Sparse Core Ops, SparseCore 0:
  28.3 123.8 all-reduce.1
where the time goes:
time: 167 us; the launch traced here: 166 us
  waiting for transfers between devices  77.7 us (47%)
  blocking collectives  56.2 us (34%)
  between operations  14.1 us (8%)
  matrix products  8.45 us (5%)
  other arithmetic  7.59 us (5%)
  local copies, waits for them, and re-layouts  2.47 us (1%)
    psum x1, waiting for transfers between devices, on_device(): right, gram = lax.psum((part_right, own_share), ('dp', 'tp'))  77.7 us
    psum x1, blocking collectives, on_device(): right, gram = lax.psum((part_right, own_share), ('dp', 'tp'))  39.5 us
    psum x1, blocking collectives, on_device(): left = lax.psum(part_left, 'dp')  16.7 us
    dot_general x1, matrix products, on_device(): jnp.einsum('lir,lrw->liw', left, mixed, precision=lax.Precision.HIGHEST)  4.38 us
  transfers between devices with their start and end apart: 1, of which 1 were waited for; matrix products, arithmetic and copies ran while one was open for 4% of the time, Pallas kernels for 0%

commit v1 on v0

--- a/solution.py
+++ b/solution.py
@@ -14,7 +14,7 @@
         right_factor.astype(jnp.bfloat16),
         preferred_element_type=jnp.float32,
     )
-    left = lax.psum(part_left, "dp")
+    left = jnp.sum(lax.all_gather(part_left, "dp"), axis=0)
     part_gram = jnp.einsum("lir,lis->lrs", left, left, precision=lax.Precision.HIGHEST)
     small_left = left.astype(jnp.bfloat16)
     part_right = jnp.einsum(

time: 167 us -> 160 us (0.958)
  blocking collectives: 56.2 us -> 48.2 us
    psum x1 -> x0, blocking collectives: 16.7 us -> none  [on_device(): left = lax.psum(part_left, 'dp')]
    all_gather x0 -> x1, blocking collectives: none -> 8.73 us  [on_device(): left = jnp.sum(lax.all_gather(part_left, 'dp'), axis=0)]
where the time goes in v1:
time: 160 us; the launch traced here: 159 us
  waiting for transfers between devices  78.5 us (49%)
  blocking collectives  48.2 us (30%)
  between operations  14.1 us (9%)
  matrix products  8.45 us (5%)
  other arithmetic  7.6 us (5%)
  local copies, waits for them, and re-layouts  2.46 us (2%)
    psum x1, waiting for transfers between devices, on_device(): right, gram = lax.psum((part_right, own_share), ('dp', 'tp'))  78.5 us
    psum x1, blocking collectives, on_device(): right, gram = lax.psum((part_right, own_share), ('dp', 'tp'))  39.5 us
    all_gather x1, blocking collectives, on_device(): left = jnp.sum(lax.all_gather(part_left, 'dp'), axis=0)  8.73 us
    dot_general x1, matrix products, on_device(): jnp.einsum('lir,lrw->liw', left, mixed, precision=lax.Precision.HIGHEST)  4.38 us
  transfers between devices with their start and end apart: 1, of which 1 were waited for; matrix products, arithmetic and copies ran while one was open for 4% of the time, Pallas kernels for 0%

profile of v1, /device:TPU:8, one launch (start us, length us, event | category | flops | bytes accessed | tf_op | source)
XLA Modules:
  0.0 159.4 jit_solution(5869844852154798901)
XLA Ops:
  7.2 0.0 copy-start
  7.2 0.0 all-reduce.2.cloned.1.call-start
  7.2 1.6 %copy-done = bf16[1,4,384,768]{3,2,1,0:T(8,128)(2,1)S(1)} copy-done((bf16[1,4,384,768]{3,2,1,0:T(8,128)(2,1)S(1)}, bf16[1,4,384,768]{3,2,1,0:T(8,128)(2,1)}, u32[]{:S(2)}) %copy-start) | copy-done | bytes 2359320
  8.8 1.6 fusion.2
  10.4 8.7 %all-gather = f32[16,384,8]{1,2,0:T(8,128)S(1)} all-gather(f32[4,384,8]{1,2,0:T(8,128)S(1)} %fusion.2), channel_id=2, replica_groups=mesh['dp'=4,'tp'=8] {'dp'}, dimensions={0}, use_global_device_ids=true | all-gather | bytes 245760 | tf_op jit(solution)/shard_map/all_gather | solution.py:17
  19.2 1.1 fusion.5
  20.2 0.0 all-reduce.2.cloned.1.call-update
  20.3 0.2 convolution_multiply_fusion.1
  20.5 0.1 copy.17
  20.6 39.5 %psum.14 = f32[4,8,8]{1,2,0:T(8,128)S(1)} all-reduce(f32[4,8,8]{1,2,0:T(8,128)S(1)} %convolution_multiply_fusion.1), channel_id=1, replica_groups=mesh['dp'=4,'tp'=8] {'dp','tp'}, use_global_device_ids=true, to_apply=%region_1.0 | all-reduce | flops 256 | bytes 2048 | tf_op jit(solution)/shard_map/psum | solution.py:24
  60.1 0.1 copy.16
  60.2 0.6 gather_fusion
  60.8 0.1 multiply_add_fusion
  60.9 0.1 copy.18
  60.9 0.1 fusion.15
  61.0 2.9 %custom-call.9 = f32[4,8,8]{2,1,0:T(8,128)S(1)} custom-call(f32[4,8,8]{2,1,0:T(8,128)S(1)} %fusion.15), custom_call_target="Cholesky" | custom-call | tf_op jit(solution)/shard_map/jit(cholesky)/cholesky | solution.py:30
  63.9 0.1 select_reduce_fusion
  64.0 0.1 compare_reduce_fusion
  64.1 0.1 select_bitcast_fusion
  64.2 2.5 %custom-call.10 = f32[4,1,8,8]{2,3,1,0:T(8,128)S(1)} custom-call(f32[4,1,8,8]{3,2,1,0:T(8,128)S(1)} %select_bitcast_fusion), custom_call_target="InvertDiagBlocksLowerTriangular" | custom-call | tf_op jit(solution)/shard_map/triangular_solve | solution.py:34
  66.7 78.5 %all-reduce.2.cloned.1.call-done = f32[4,768,8]{1,2,0:T(8,128)} async-done(((f32[4,768,8]{1,2,0:T(8,128)}), f32[4,768,8]{1,2,0:T(8,128)}) %all-reduce.2.cloned.1.call-update) | async-done | bytes 98320 | tf_op jit(solution)/shard_map/psum | solution.py:24
  145.2 1.0 multiply_reduce_fusion
  146.2 1.1 fusion.9
  147.3 0.2 fusion.12
  147.4 0.0 copy-start.1
  147.4 4.4 %multiply_subtract_fusion = (f32[4,384,192]{1,2,0:T(8,128)}, f32[4,384,192]{1,2,0:T(8,128)}) fusion(f32[4,384,192]{1,2,0:T(8,128)} %param.6, f32[4,384,8]{1,2,0:T(8,128)S(1)} %reduce_sum.27, f32[4,8,192]{2,1,0:T(8,128)S(1)} %fusion.12, f32[4,384,192]{1,2,0:T(8,128)} %param.7), kind=kOutput, calls=%fused_computation.7 | convolution fusion | flops 29786112 | bytes 4792320 | tf_op jit(solution)/shard_map/lir,lrw->liw/dot_general | solution.py:35
  151.8 0.0 copy-done.1
  151.8 0.7 broadcast_multiply_fusion
  (8 shorter events, 0.1 us)
Async XLA Ops:
  7.2 1.7 %copy-start = (bf16[1,4,384,768]{3,2,1,0:T(8,128)(2,1)S(1)}, bf16[1,4,384,768]{3,2,1,0:T(8,128)(2,1)}, u32[]{:S(2)}) copy-start(bf16[1,4,384,768]{3,2,1,0:T(8,128)(2,1)} %param.4) | copy-start | bytes 7077892
  7.2 138.0 %all-reduce.2.cloned.1.call-start = ((), (), s32[]{:S(2)}) async-start(), calls=%async_computation | async-start | bytes 196608 | tf_op jit(solution)/shard_map/psum | solution.py:24
  147.4 4.4 %copy-start.1 = (f32[4,768,8]{1,2,0:T(8,128)S(1)}, f32[4,768,8]{1,2,0:T(8,128)}, u32[]{:S(2)}) copy-start(f32[4,768,8]{1,2,0:T(8,128)} %all-reduce.2.cloned.1.call-done) | copy-start | bytes 294916
Sparse Core Ops, SparseCore 0:
  20.4 124.7 all-reduce.1
